TPU v7x, 32 devices: a whole 2x2x4 slice. The times are simulated.
32 devices in a mesh: gx: 4 (over y, x), gy: 8 (over z, core).
Axes of the slice: x: 2, y: 2, z: 4, core: 2. Of those that a mesh axis runs over, the one named last changes fastest.
Arguments:
- fine_nodes: bfloat16 [65536, 256], P(('gx', 'gy')), may hold values from -6 to 6
- fine_weights: bfloat16 [6, 256, 256], replicated, may hold values from -0.375 to 0.375
- coarse_weights: bfloat16 [6, 256, 256], replicated, may hold values from -0.375 to 0.375
- top_weights: bfloat16 [6, 256, 256], replicated, may hold values from -0.375 to 0.375
- gains: float32 [3, 256], replicated, may hold values from 0.1 to 1.9
- send_list: int32 [4, 8, 4, 512], P('gx', 'gy'), may hold values from 0 to 2047
- fine_sender: int32 [4, 8, 8192], P('gx', 'gy'), may hold values from 0 to 4095, as said below
- fine_receiver: int32 [4, 8, 8192], P('gx', 'gy'), may hold values from 0 to 2048, as said below
- pool_owner: int32 [65536, 1], P(('gx', 'gy')), may hold values from 0 to 3; in each aligned block of 2048 rows (0 to 2047, 2048 to 4095, ...) at most 1024 rows name the same one
- pool_local: int32 [65536], P(('gx', 'gy')), may hold values from 0 to 255
- coarse_sender: int32 [8, 4096], P('gy', 'gx'), may hold values from 0 to 1023
- coarse_receiver: int32 [8, 4096], P('gy', 'gx'), may hold values from 0 to 255
- top_parent: int32 [8, 1024], P('gy', 'gx'), may hold values from 0 to 127
- top_sender: int32 [8, 512], P('gy'), may hold values from 0 to 127
- top_receiver: int32 [8, 512], P('gy'), may hold values from 0 to 127
Outputs:
- fine_state: bfloat16 [65536, 256], P(('gx', 'gy'))
- coarse_state: bfloat16 [8, 1024, 256], P('gy', 'gx')
Inputs may be any that keep to these rules, and one draw needn't show every extreme that they name: `fine_sender`: values below 2048 name the device's own nodes; larger values name a halo row of a neighbour that exists. `fine_receiver`: 2048 marks an empty slot; a device's live slots come first, and some device has no empty slot. `pool_owner`: among the rows of one device no member is named more than 1024 times.
All inputs are finite; a program needn't handle non-finite values.
Results may differ from a plain program's by a relative error of at most 0.015.
Values may be sent and summed in bfloat16 or wider, within the bound.
No kernel may reach another device: no remote copies, remote signals or barrier semaphores. Data moves between devices by JAX's collectives and lax.ppermute only.
A program may use at most 64 MiB of HBM per device.

v0:
```python
import math
import jax
import jax.numpy as jnp
from jax import lax
from jax.sharding import PartitionSpec as P


def passed_along(block, axis, distance):
    devices = range(lax.axis_size(axis))
    route = [(i - distance, i) for i in devices if i - distance in devices]
    return lax.ppermute(block, axis, route)


def project(states, weights):
    sender_term = jnp.dot(states, weights[0], preferred_element_type=jnp.float32).astype(
        jnp.bfloat16
    )
    receiver_term = jnp.dot(states, weights[1], preferred_element_type=jnp.float32).astype(
        jnp.bfloat16
    )
    return (sender_term, receiver_term)


def gather_messages(fetch, receiver_term, receivers, weight_out, count, most):
    edges = receivers.shape[0]
    block = math.gcd(edges, most)
    width = receiver_term.shape[1]

    def advance(summed, turn):
        begin = turn * block
        targets = lax.dynamic_slice_in_dim(receivers, begin, block)
        before = fetch(begin, block) + jnp.take(
            receiver_term, jnp.minimum(targets, count - 1), axis=0
        ).astype(jnp.float32)
        hidden = jax.nn.silu(before).astype(jnp.bfloat16)
        message = jnp.dot(hidden, weight_out, preferred_element_type=jnp.float32)
        return (summed.at[targets].add(message, mode="drop"), None)

    turns = jnp.arange(edges // block, dtype=jnp.int32)
    summed, unused = lax.scan(advance, jnp.zeros((count, width), jnp.float32), turns)
    return summed


def update_nodes(states, aggregate, weights, gain):
    merged = jnp.dot(states, weights[3], preferred_element_type=jnp.float32)
    merged = merged + jnp.dot(
        aggregate.astype(jnp.bfloat16), weights[4], preferred_element_type=jnp.float32
    )
    inner = jax.nn.silu(merged).astype(jnp.bfloat16)
    output = jnp.dot(inner, weights[5], preferred_element_type=jnp.float32)
    centred = output - jnp.mean(output, axis=1, keepdims=True)
    spread = jnp.mean(centred * centred, axis=1, keepdims=True)
    return (states.astype(jnp.float32) + gain * centred * lax.rsqrt(spread + 1e-05)).astype(
        jnp.bfloat16
    )


def table_fetch(table, senders):

    def fetch(begin, rows):
        picked = lax.dynamic_slice_in_dim(senders, begin, rows)
        return jnp.take(table, picked, axis=0).astype(jnp.float32)

    return fetch


def body(
    fine_nodes,
    fine_weights,
    coarse_weights,
    top_weights,
    gains,
    send_list,
    fine_sender,
    fine_receiver,
    pool_owner,
    pool_local,
    coarse_sender,
    coarse_receiver,
    top_parent,
    top_sender,
    top_receiver,
):
    nodes = fine_nodes.shape[0]
    width = fine_nodes.shape[1]
    members = lax.axis_size("gx")
    coarse_rows = nodes // 8
    top_rows = coarse_rows * members // 8
    lists = send_list.reshape(4, -1)
    fine_send, fine_recv = project(fine_nodes, fine_weights)
    pieces = [fine_send]
    for slot, offset in ((0, 1), (1, -1)):
        pieces.append(passed_along(jnp.take(fine_send, lists[slot], axis=0), "gx", offset))
    for slot, offset in ((2, 1), (3, -1)):
        pieces.append(passed_along(jnp.take(fine_send, lists[slot], axis=0), "gy", offset))
    table = jnp.concatenate(pieces, axis=0)
    fine_aggregate = gather_messages(
        table_fetch(table, fine_sender.reshape(-1)),
        fine_recv,
        fine_receiver.reshape(-1),
        fine_weights[2],
        nodes,
        4096,
    )
    fine_one = update_nodes(fine_nodes, fine_aggregate, fine_weights, gains[0])
    owner = pool_owner.reshape(-1)
    parent = owner * coarse_rows + pool_local
    partial_value = (
        jnp.zeros((members * coarse_rows, width), jnp.float32)
        .at[parent]
        .add(fine_one.astype(jnp.float32))
    )
    partial_count = jnp.zeros((members * coarse_rows,), jnp.float32).at[parent].add(1.0)
    coarse_sum, child_count = (
        lax.psum_scatter(
            partial_value.astype(jnp.bfloat16), "gx", scatter_dimension=0, tiled=True
        ).astype(jnp.float32),
        lax.psum_scatter(
            partial_count.astype(jnp.bfloat16), "gx", scatter_dimension=0, tiled=True
        ).astype(jnp.float32),
    )
    coarse_zero = (coarse_sum / jnp.maximum(child_count, 1.0)[:, None]).astype(jnp.bfloat16)
    coarse_send, coarse_recv = project(coarse_zero, coarse_weights)
    coarse_senders = coarse_sender.reshape(-1)
    piece = lax.all_gather(coarse_send, "gx", axis=0, tiled=True)
    inside = (coarse_senders >= 0) & (coarse_senders < piece.shape[0])
    picked = jnp.take(piece, jnp.clip(coarse_senders, 0, piece.shape[0] - 1), axis=0).astype(
        jnp.float32
    )
    gathered = jnp.where(inside[:, None], picked, 0.0)

    def slice_gathered(begin, rows):
        return gathered

    coarse_aggregate = gather_messages(
        slice_gathered,
        coarse_recv,
        coarse_receiver.reshape(-1),
        coarse_weights[2],
        coarse_rows,
        4096,
    )
    coarse_one = update_nodes(coarse_zero, coarse_aggregate, coarse_weights, gains[1])
    parents = top_parent.reshape(-1)
    partial_top = (
        jnp.zeros((top_rows, width), jnp.float32).at[parents].add(coarse_one.astype(jnp.float32))
    )
    partial_top_count = jnp.zeros((top_rows,), jnp.float32).at[parents].add(1.0)
    top_sum, top_count = (
        lax.psum(partial_top.astype(jnp.bfloat16), "gx").astype(jnp.float32),
        lax.psum(partial_top_count.astype(jnp.bfloat16), "gx").astype(jnp.float32),
    )
    top_zero = (top_sum / jnp.maximum(top_count, 1.0)[:, None]).astype(jnp.bfloat16)
    top_send, top_recv = project(top_zero, top_weights)
    top_aggregate = gather_messages(
        table_fetch(top_send, top_sender.reshape(-1)),
        top_recv,
        top_receiver.reshape(-1),
        top_weights[2],
        top_rows,
        4096,
    )
    top_one = update_nodes(top_zero, top_aggregate, top_weights, gains[2])
    coarse_two = (
        coarse_one.astype(jnp.float32) + jnp.take(top_one, parents, axis=0).astype(jnp.float32)
    ).astype(jnp.bfloat16)
    whole = lax.all_gather(coarse_two, "gx", axis=0, tiled=True)
    lifted = jnp.take(whole, parent, axis=0)
    fine_state = (fine_one.astype(jnp.float32) + lifted.astype(jnp.float32)).astype(jnp.bfloat16)
    return (fine_state, coarse_two[None])


def solution(mesh):
    placed = (
        P(("gx", "gy"), None),
        P(),
        P(),
        P(),
        P(),
        P("gx", "gy", None, None),
        P("gx", "gy", None),
        P("gx", "gy", None),
        P(("gx", "gy"), None),
        P(("gx", "gy")),
        P("gy", "gx"),
        P("gy", "gx"),
        P("gy", "gx"),
        P("gy", None),
        P("gy", None),
    )
    return jax.shard_map(
        body,
        mesh=mesh,
        in_specs=placed,
        out_specs=(P(("gx", "gy"), None), P("gy", "gx", None)),
        check_vma=False,
    )
```

profile of v0, /device:TPU:0, one launch (start us, length us, event | category | flops | bytes accessed | tf_op | source)
XLA Modules:
  0.0 395.7 jit_solution(5768898327504365994)
XLA Ops:
  12.6 5.6 %collective-permute-start = (bf16[512,256]{1,0:T(8,128)(2,1)}, bf16[512,256]{1,0:T(8,128)(2,1)}, u32[]{:S(2)}, u32[]{:S(2)}) collective-permute-start(bf16[512,256]{1,0:T(8,128)(2,1)} %broadcast_select_fusion.3), channel_id=1, source_target_pairs={{0,8},{8,16},{16,24},{1,9},{9,17},{17,25},{2,10},{10,18},{18,26},{... | collective-permute-start | bytes 786440 | tf_op jit(solution)/shard_map/ppermute | solution.py:11
  25.1 2.1 collective-permute-start.2
  34.7 2.7 fusion.46
  41.0 14.7 %scatter_custom_fusion.2 = f32[1024]{0:T(1024)S(1)} fusion(s32[2048]{0:T(1024)S(1)} %get-tuple-element.111, f32[2048]{0:T(1024)S(1)} %broadcast.313, f32[]{:T(128)} %constant.135.clone.1), kind=kCustom, calls=%fused_computation.167 | custom fusion | flops 2048 | bytes 4100 | tf_op jit(solution)/shard_map/scatter-add | solution.py:113
  55.7 2.3 scatter_custom_fusion.5
  59.2 11.6 %all-reduce.1 = (bf16[1024]{0:T(1024)(128)(2,1)}, bf16[128]{0:T(256)(128)(2,1)S(1)}) all-reduce(bf16[1024]{0:T(1024)(128)(2,1)S(1)} %convert_element_type.145, bf16[128]{0:T(256)(128)(2,1)S(1)} %convert_element_type.160), channel_id=3, replica_groups=mesh['gx'=4,'gy'=8] {'gx'}, use_global_device_ids=true, to_apply=%region_8.10.clone | all-reduce | flops 1152 | bytes 4608
  71.9 2.3 copy.34
  80.1 131.3 %while.2 = (s32[]{:T(128)}, f32[2048,256]{1,0:T(8,128)S(1)}, s32[2]{0:T(128)S(1)}, s32[8192]{0:T(1024)S(1)}, s32[8192]{0:T(1024)S(1)}, /*index=5*/bf16[4096,256]...) while((s32[]{:T(128)}, f32[2048,256]{1,0:T(8,128)S(1)}, ...), condition=%wide.region_2.4_spmd, body=%wide.region_0.3_spmd.sunk | while | flops 548507648 | bytes 30195924 | solution.py:40
  81.3 17.0 %gather_fusion = bf16[4096,256]{1,0:T(8,128)(2,1)} fusion(bf16[2048,256]{1,0:T(8,128)(2,1)S(1)} %get-tuple-element.235, s32[4096]{0:T(1024)S(1)} %get-tuple-element.201), kind=kCustom, calls=%fused_computation.2.clone.1 | custom fusion | bytes 4210688 | tf_op jit(solution)/shard_map/while/body/eval_jaxpr/jit(_take)/gather | solution.py:32
  98.3 17.7 %gather_fusion.1 = bf16[4096,256]{1,0:T(8,128)(2,1)} fusion(bf16[4096,256]{1,0:T(8,128)(2,1)} %get-tuple-element.234, s32[4096]{0:T(1024)S(1)} %get-tuple-element.202), kind=kCustom, calls=%fused_computation.1.clone.1 | custom fusion | bytes 4210688 | tf_op jit(solution)/shard_map/while/body/eval_jaxpr/jit(_take)/gather | solution.py:62
  116.0 6.1 %fusion.123 = f32[4096,256]{1,0:T(8,128)} fusion(bf16[256,256]{1,0:T(8,128)(2,1)S(1)} %copy-done.6, bf16[4096,256]{1,0:T(8,128)(2,1)} %gather_fusion, bf16[4096,256]{1,0:T(8,128)(2,1)} %gather_fusion.1, pred[4096]{0:T(1024)(128)(4,1)S(1)} %get-tuple-element.203, pred[4096]{0:T(1024)(128)(4,1)S(1)} %get-tuple-element.204), kind=kOutput, calls=%fused_computation.20.clone.1 | convolution fusion | flops 547356672 | bytes 8527872 | tf_op jit(solution)/shard_map/while/body/eval_jaxpr/dot_general | solution.py:36
  122.2 23.6 %scatter_fusion = f32[2048,256]{1,0:T(8,128)S(1)} fusion(f32[2048,256]{1,0:T(8,128)S(1)} %get-tuple-element.218, s32[4096]{0:T(1024)S(1)} %get-tuple-element.200, f32[4096,256]{1,0:T(8,128)} %fusion.123), kind=kCustom, calls=%fused_computation.12.clone.1 | custom fusion | flops 1048576 | bytes 12599296 | tf_op jit(solution)/shard_map/while/body/eval_jaxpr/scatter-add | solution.py:37
  147.0 17.0 %gather_fusion = bf16[4096,256]{1,0:T(8,128)(2,1)} fusion(bf16[2048,256]{1,0:T(8,128)(2,1)S(1)} %get-tuple-element.235, s32[4096]{0:T(1024)S(1)} %get-tuple-element.201), kind=kCustom, calls=%fused_computation.2.clone.1 | custom fusion | bytes 4210688 | tf_op jit(solution)/shard_map/while/body/eval_jaxpr/jit(_take)/gather | solution.py:32
  163.9 17.7 %gather_fusion.1 = bf16[4096,256]{1,0:T(8,128)(2,1)} fusion(bf16[4096,256]{1,0:T(8,128)(2,1)} %get-tuple-element.234, s32[4096]{0:T(1024)S(1)} %get-tuple-element.202), kind=kCustom, calls=%fused_computation.1.clone.1 | custom fusion | bytes 4210688 | tf_op jit(solution)/shard_map/while/body/eval_jaxpr/jit(_take)/gather | solution.py:62
  181.7 6.1 %fusion.123 = f32[4096,256]{1,0:T(8,128)} fusion(bf16[256,256]{1,0:T(8,128)(2,1)S(1)} %copy-done.6, bf16[4096,256]{1,0:T(8,128)(2,1)} %gather_fusion, bf16[4096,256]{1,0:T(8,128)(2,1)} %gather_fusion.1, pred[4096]{0:T(1024)(128)(4,1)S(1)} %get-tuple-element.203, pred[4096]{0:T(1024)(128)(4,1)S(1)} %get-tuple-element.204), kind=kOutput, calls=%fused_computation.20.clone.1 | convolution fusion | flops 547356672 | bytes 8527872 | tf_op jit(solution)/shard_map/while/body/eval_jaxpr/dot_general | solution.py:36
  187.8 23.6 %scatter_fusion = f32[2048,256]{1,0:T(8,128)S(1)} fusion(f32[2048,256]{1,0:T(8,128)S(1)} %get-tuple-element.218, s32[4096]{0:T(1024)S(1)} %get-tuple-element.200, f32[4096,256]{1,0:T(8,128)} %fusion.123), kind=kCustom, calls=%fused_computation.12.clone.1 | custom fusion | flops 1048576 | bytes 12599296 | tf_op jit(solution)/shard_map/while/body/eval_jaxpr/scatter-add | solution.py:37
  211.5 3.8 fusion.99
  221.1 13.0 %scatter_custom_fusion.1 = f32[1024,256]{1,0:T(8,128)} fusion(s32[2048]{0:T(1024)S(1)} %copy-done.11, f32[2048,256]{1,0:T(8,128)} %copy.35, f32[]{:T(128)} %constant.135.clone.1), kind=kCustom, calls=%fused_computation.52 | custom fusion | flops 524288 | bytes 1049088 | tf_op jit(solution)/shard_map/scatter-add | solution.py:111
  234.1 2.2 copy.36
  237.2 26.1 %reduce-scatter.2.cloned.1.call-done = bf16[256,256]{0,1:T(8,128)(2,1)} async-done(((bf16[1024,256]{0,1:T(8,128)(2,1)}), bf16[256,256]{0,1:T(8,128)(2,1)}) %reduce-scatter.2.cloned.1.call-update) | async-done | bytes 131088 | tf_op jit(solution)/shard_map/reduce_scatter | solution.py:115
  264.6 10.5 %all_gather.6 = bf16[1024,256]{1,0:T(8,128)(2,1)S(1)} all-gather(bf16[256,256]{1,0:T(8,128)(2,1)S(1)} %convolution_convert_fusion.3), channel_id=1, replica_groups=mesh['gx'=4,'gy'=8] {'gx'}, dimensions={0}, use_global_device_ids=true | all-gather | bytes 655360 | tf_op jit(solution)/shard_map/all_gather | solution.py:125
  275.1 3.9 gather_fusion.2
  280.2 5.0 %gather_fusion.3 = bf16[1024,256]{1,0:T(8,128)(2,1)} fusion(bf16[256,256]{1,0:T(8,128)(2,1)S(1)} %convolution_convert_fusion.2, s32[1024]{0:T(1024)S(1)} %get-tuple-element.140), kind=kCustom, calls=%fused_computation.9 | custom fusion | bytes 1052672 | tf_op jit(solution)/shard_map/while/body/eval_jaxpr/jit(_take)/gather | solution.py:32
  285.1 2.7 fusion.15
  287.8 6.6 %scatter_custom_fusion.3 = f32[256,256]{1,0:T(8,128)S(1)} fusion(s32[1024]{0:T(1024)S(1)} %bitcast.137, f32[1024,256]{1,0:T(8,128)} %fusion.15, f32[]{:T(128)} %constant.135.clone.1), kind=kCustom, calls=%fused_computation.112 | custom fusion | flops 262144 | bytes 262656 | tf_op jit(solution)/shard_map/while/body/eval_jaxpr/scatter-add | solution.py:37
  300.8 42.0 %all-reduce.4.cloned.1.call-done = bf16[128,256]{1,0:T(8,128)(2,1)} async-done(((bf16[128,256]{1,0:T(8,128)(2,1)}), bf16[128,256]{1,0:T(8,128)(2,1)}) %all-reduce.4.cloned.1.call-update) | async-done | bytes 65552 | tf_op jit(solution)/shard_map/psum | solution.py:150
  351.1 4.1 %scatter_custom_fusion.6 = f32[128,256]{1,0:T(8,128)S(1)} fusion(s32[512]{0:T(512)} %bitcast.142, f32[512,256]{1,0:T(8,128)} %fusion.21, f32[]{:T(128)} %constant.135.clone.1), kind=kCustom, calls=%fused_computation.123 | custom fusion | flops 131072 | bytes 131584 | tf_op jit(solution)/shard_map/while/body/eval_jaxpr/scatter-add | solution.py:37
  359.4 12.5 %all_gather.7 = bf16[1024,256]{0,1:T(8,128)(2,1)S(1)} all-gather(bf16[256,256]{0,1:T(8,128)(2,1)S(1)} %add_convert_fusion.2), channel_id=1, replica_groups=mesh['gx'=4,'gy'=8] {'gx'}, dimensions={0}, use_global_device_ids=true | all-gather | bytes 655360 | tf_op jit(solution)/shard_map/all_gather | solution.py:167
  372.0 9.1 %gather_fusion.5 = bf16[2048,256]{1,0:T(8,128)(2,1)} fusion(bf16[1024,256]{1,0:T(8,128)(2,1)S(1)} %copy.39, s32[2048]{0:T(1024)S(1)} %broadcast_clamp_fusion), kind=kCustom, calls=%fused_computation.11 | custom fusion | bytes 2105344 | tf_op jit(solution)/shard_map/jit(_take)/gather | solution.py:168
  381.1 2.3 copy.40
  383.4 2.5 add_convert_fusion
  385.9 2.3 copy.41
  (177 shorter events, 60.5 us)
Async XLA Ops:
  7.2 256.2 %reduce-scatter.2.cloned.1.call-start = ((), (), s32[]{:S(2)}) async-start(), calls=%async_computation.1 | async-start | bytes 655360 | tf_op jit(solution)/shard_map/reduce_scatter | solution.py:115
  12.6 63.0 %collective-permute-start = (bf16[512,256]{1,0:T(8,128)(2,1)}, bf16[512,256]{1,0:T(8,128)(2,1)}, u32[]{:S(2)}, u32[]{:S(2)}) collective-permute-start(bf16[512,256]{1,0:T(8,128)(2,1)} %broadcast_select_fusion.3), channel_id=1, source_target_pairs={{0,8},{8,16},{16,24},{1,9},{9,17},{17,25},{2,10},{10,18},{18,26},{... | collective-permute-start | bytes 786440 | tf_op jit(solution)/shard_map/ppermute | solution.py:11
  21.0 55.6 %collective-permute-start.1 = (bf16[512,256]{1,0:T(8,128)(2,1)}, bf16[512,256]{1,0:T(8,128)(2,1)}, u32[]{:S(2)}, u32[]{:S(2)}) collective-permute-start(bf16[512,256]{1,0:T(8,128)(2,1)} %broadcast_select_fusion.2), channel_id=1, source_target_pairs={{8,0},{16,8},{24,16},{9,1},{17,9},{25,17},{10,2},{18,10},{26,18},{... | collective-permute-start | bytes 786440 | tf_op jit(solution)/shard_map/ppermute | solution.py:11
  25.1 52.5 %collective-permute-start.2 = (bf16[512,256]{1,0:T(8,128)(2,1)}, bf16[512,256]{1,0:T(8,128)(2,1)}, u32[]{:S(2)}, u32[]{:S(2)}) collective-permute-start(bf16[512,256]{1,0:T(8,128)(2,1)} %broadcast_select_fusion.1), channel_id=1, source_target_pairs={{0,1},{1,2},{2,3},{3,4},{4,5},{5,6},{6,7},{8,9},{9,10},{10,11},{11... | collective-permute-start | bytes 786440 | tf_op jit(solution)/shard_map/ppermute | solution.py:11
  29.2 5.5 %copy-start.1 = (bf16[2048,256]{1,0:T(8,128)(2,1)S(1)}, bf16[2048,256]{1,0:T(8,128)(2,1)}, u32[]{:S(2)}) copy-start(bf16[2048,256]{1,0:T(8,128)(2,1)} %param.21) | copy-start | bytes 3145732
  30.1 48.5 %collective-permute-start.3 = (bf16[512,256]{1,0:T(8,128)(2,1)}, bf16[512,256]{1,0:T(8,128)(2,1)S(1)}, u32[]{:S(2)}, u32[]{:S(2)}) collective-permute-start(bf16[512,256]{1,0:T(8,128)(2,1)} %broadcast_select_fusion), channel_id=1, source_target_pairs={{1,0},{2,1},{3,2},{4,3},{5,4},{6,5},{7,6},{9,8},{10,9},{11,10},{12... | collective-permute-start | bytes 786440 | tf_op jit(solution)/shard_map/ppermute | solution.py:11
  33.0 5.6 %copy-start.23 = (s32[1,512]{1,0:T(1,128)S(1)}, s32[1,512]{1,0:T(1,128)}, u32[]{:S(2)}) copy-start(s32[1,512]{1,0:T(1,128)} %param.35) | copy-start | bytes 6148
  33.1 5.6 %copy-start.22 = (s32[1,512]{1,0:T(1,128)S(1)}, s32[1,512]{1,0:T(1,128)}, u32[]{:S(2)}) copy-start(s32[1,512]{1,0:T(1,128)} %param.34) | copy-start | bytes 6148
  33.1 6.7 %copy-start.29 = (f32[3,256]{1,0:T(4,128)S(1)}, f32[3,256]{1,0:T(4,128)}, u32[]{:S(2)}) copy-start(f32[3,256]{1,0:T(4,128)} %param.25) | copy-start | bytes 9220
  33.1 7.3 %copy-start.20 = (s32[2048,1]{0,1:T(1,128)S(1)}, s32[2048,1]{0,1:T(1,128)}, u32[]{:S(2)}) copy-start(s32[2048,1]{0,1:T(1,128)} %param.29) | copy-start | bytes 24580
  33.1 7.3 %copy-start.21 = (s32[2048]{0:T(1024)S(1)}, s32[2048]{0:T(1024)}, u32[]{:S(2)}) copy-start(s32[2048]{0:T(1024)} %param.30) | copy-start | bytes 24580
  33.1 22.6 %copy-start.30 = (s32[1,256]{1,0:T(1,128)S(1)}, s32[1,256]{1,0:T(1,128)}, u32[]{:S(2)}) copy-start(s32[1,256]{1,0:T(1,128)} %param.33) | copy-start | bytes 3076
  33.1 24.9 %copy-start.12 = (s32[1,1024]{1,0:T(1,128)S(1)}, s32[1,1024]{1,0:T(1,128)}, u32[]{:S(2)}) copy-start(s32[1,1024]{1,0:T(1,128)} %param.32) | copy-start | bytes 12292
  34.7 39.5 %copy-start.35 = (u32[32]{0:T(128)S(1)}, u32[32]{0:T(128)}, u32[]{:S(2)}) copy-start(u32[32]{0:T(128)} %constant.209) | copy-start | bytes 388
  41.0 37.6 %copy-start.10 = (s32[2048]{0:T(1024)}, s32[2048]{0:T(1024)S(1)}, u32[]{:S(2)}) copy-start(s32[2048]{0:T(1024)S(1)} %get-tuple-element.111) | copy-start | bytes 24580
  55.7 22.9 %copy-start.26 = (s32[256,1]{0,1:T(1,128)}, s32[256,1]{0,1:T(1,128)S(1)}, u32[]{:S(2)}) copy-start(s32[256,1]{0,1:T(1,128)S(1)} %compare_select_fusion.10) | copy-start | bytes 3076
  75.6 4.5 %copy-start.3 = (s32[1,1,8192]{2,1,0:T(1,128)S(1)}, s32[1,1,8192]{2,1,0:T(1,128)}, u32[]{:S(2)}) copy-start(s32[1,1,8192]{2,1,0:T(1,128)} %param.28) | copy-start | bytes 98308
  75.6 4.5 %copy-start.4 = (s32[1,1,8192]{2,1,0:T(1,128)S(1)}, s32[1,1,8192]{2,1,0:T(1,128)}, u32[]{:S(2)}) copy-start(s32[1,1,8192]{2,1,0:T(1,128)} %param.27) | copy-start | bytes 98308
  98.3 17.8 %copy-start.6 = (bf16[256,256]{1,0:T(8,128)(2,1)S(1)}, bf16[256,256]{1,0:T(8,128)(2,1)}, u32[]{:S(2)}) copy-start(bf16[256,256]{1,0:T(8,128)(2,1)} %get-tuple-element.236) | copy-start | bytes 393220 | tf_op jit(solution)/shard_map/while
  163.9 17.8 %copy-start.6 = (bf16[256,256]{1,0:T(8,128)(2,1)S(1)}, bf16[256,256]{1,0:T(8,128)(2,1)}, u32[]{:S(2)}) copy-start(bf16[256,256]{1,0:T(8,128)(2,1)} %get-tuple-element.236) | copy-start | bytes 393220 | tf_op jit(solution)/shard_map/while
  221.1 16.0 %copy-start.9 = (s32[1,1024]{1,0:T(1,128)S(1)}, s32[1,1024]{1,0:T(1,128)}, u32[]{:S(2)}) copy-start(s32[1,1024]{1,0:T(1,128)} %param.31) | copy-start | bytes 12292
  221.1 16.0 %copy-start.14 = (s32[1,1024]{1,0:T(1,128)S(1)}, s32[1,1024]{1,0:T(1,128)}, u32[]{:S(2)}) copy-start(s32[1,1024]{1,0:T(1,128)} %broadcast_clamp_fusion.3) | copy-start | bytes 12292
  221.1 16.0 %copy-start.15 = (s32[1,1024]{1,0:T(1,128)S(1)}, s32[1,1024]{1,0:T(1,128)}, u32[]{:S(2)}) copy-start(s32[1,1024]{1,0:T(1,128)} %broadcast_minimum_fusion) | copy-start | bytes 12292
  221.1 16.1 %copy-start.13 = (s32[1,1024]{1,0:T(1,128)S(1)}, s32[1,1024]{1,0:T(1,128)}, u32[]{:S(2)}) copy-start(s32[1,1024]{1,0:T(1,128)} %param.32) | copy-start | bytes 12292
  221.1 16.1 %copy-start.16 = (s32[1024,1]{0,1:T(1,128)S(1)}, s32[1024,1]{0,1:T(1,128)}, u32[]{:S(2)}) copy-start(s32[1024,1]{0,1:T(1,128)} %compare_select_fusion.4) | copy-start | bytes 12292
  236.3 106.4 %all-reduce.4.cloned.1.call-start = ((), (), s32[]{:S(2)}) async-start(), calls=%async_computation.2 | async-start | bytes 131072 | tf_op jit(solution)/shard_map/psum | solution.py:150
  287.8 10.0 %copy-start.25 = (f32[1,256]{1,0:T(1,128)S(1)}, f32[1,256]{1,0:T(1,128)}, u32[]{:S(2)}) copy-start(f32[1,256]{1,0:T(1,128)} %get-tuple-element.123) | copy-start | bytes 3076
  294.4 48.3 %copy-start.32 = (f32[128]{0:T(128)S(1)}, f32[128]{0:T(128)}, u32[]{:S(2)}) copy-start(f32[128]{0:T(128)} %convert_maximum_fusion.1) | copy-start | bytes 1540
  296.3 47.6 %copy-start.18 = (s32[1024]{0:T(1024)S(1)}, s32[1024]{0:T(1024)}, u32[]{:S(2)}) copy-start(s32[1024]{0:T(1024)} %get-tuple-element.135) | copy-start | bytes 12292
  298.1 48.9 %copy-start.17 = (s32[1024]{0:T(1024)S(1)}, s32[1024]{0:T(1024)}, u32[]{:S(2)}) copy-start(s32[1024]{0:T(1024)} %get-tuple-element.134) | copy-start | bytes 12292
  349.0 8.9 %copy-start.24 = (f32[1,256]{1,0:T(1,128)S(1)}, f32[1,256]{1,0:T(1,128)}, u32[]{:S(2)}) copy-start(f32[1,256]{1,0:T(1,128)} %get-tuple-element.121) | copy-start | bytes 3076
  351.1 8.2 %copy-start.31 = (pred[256]{0:T(512)(128)(4,1)S(1)}, pred[256]{0:T(512)(128)(4,1)}, u32[]{:S(2)}) copy-start(pred[256]{0:T(512)(128)(4,1)} %compare_and_fusion.11) | copy-start | bytes 772
  (11 other events, 31.3 us)
Sparse Core Ops, SparseCore 0:
  236.4 26.8 reduce-scatter.1
  300.9 41.8 all-reduce.3
where the time goes:
time: 397 us; the launch traced here: 396 us
  local copies, waits for them, and re-layouts  122 us (31%)
  other arithmetic  107 us (27%)
  waiting for transfers between devices  68.2 us (17%)
  matrix products  37.3 us (9%)
  blocking collectives  34.5 us (9%)
  between operations  15.5 us (4%)
  starting transfers between devices  10.4 us (3%)
    scatter-add x4, other arithmetic, advance(): return (summed.at[targets].add(message, mode='drop'), None)  57.9 us
    psum x1, waiting for transfers between devices, body(): lax.psum(partial_top.astype(jnp.bfloat16), 'gx').astype(jnp.float32)  42 us
    gather x4, local copies, waits for them, and re-layouts, advance(): jnp.take(receiver_term, jnp.minimum(targets, count - 1), axis=0)  40.8 us
    gather x3, local copies, waits for them, and re-layouts, fetch(): return jnp.take(table, picked, axis=0).astype(jnp.float32)  37.4 us
    reduce_scatter x1, waiting for transfers between devices, body(): lax.psum_scatter(partial_value.astype(jnp.bfloat16), 'gx', scatter_dimens...  26.1 us
    dot_general x4, matrix products, advance(): message = jnp.dot(hidden, weight_out, preferred_element_type=jnp.float32)  17 us
    scatter-add x1, other arithmetic, body(): jnp.zeros((members * coarse_rows,), jnp.float32).at[parent].add(1.0)  14.7 us
    scatter-add x1, other arithmetic, body(): partial_value = jnp.zeros((members * coarse_rows, width), jnp.float32).at...  13 us
  transfers between devices with their start and end apart: 6, of which 2 were waited for; matrix products, arithmetic and copies ran while one was open for 11% of the time, Pallas kernels for 0%

commit v1 on v0

--- a/solution.py
+++ b/solution.py
@@ -147,7 +147,7 @@
     )
     partial_top_count = jnp.zeros((top_rows,), jnp.float32).at[parents].add(1.0)
     top_sum, top_count = (
-        lax.psum(partial_top.astype(jnp.bfloat16), "gx").astype(jnp.float32),
+        lax.all_gather(partial_top.astype(jnp.bfloat16), "gx").sum(axis=0).astype(jnp.float32),
         lax.psum(partial_top_count.astype(jnp.bfloat16), "gx").astype(jnp.float32),
     )
     top_zero = (top_sum / jnp.maximum(top_count, 1.0)[:, None]).astype(jnp.bfloat16)

time: 397 us -> 363 us (0.914)
  waiting for transfers between devices: 68.2 us -> 26.2 us
  blocking collectives: 34.5 us -> 42.2 us
    psum x1 -> x0, waiting for transfers between devices: 42 us -> none  [body(): lax.psum(partial_top.astype(jnp.bfloat16), 'gx').astype(jnp.float32)]
    all_gather x0 -> x1, blocking collectives: none -> 7.77 us  [body(): lax.all_gather(partial_top.astype(jnp.bfloat16), 'gx').sum(axis=0)]
    unnamed x77 -> x73, local copies, waits for them, and re-layouts: 10.6 us -> 10.6 us
  transfers between devices with their start and end apart: 6 -> 5, of which waited for: 2 -> 1; matrix products, arithmetic and copies ran while one was open for 11% -> 12% of each run, Pallas kernels for 0% -> 0%
where the time goes in v1:
time: 363 us; the launch traced here: 361 us
  local copies, waits for them, and re-layouts  123 us (34%)
  other arithmetic  107 us (29%)
  blocking collectives  42.2 us (12%)
  matrix products  36.4 us (10%)
  waiting for transfers between devices  26.2 us (7%)
  between operations  15.5 us (4%)
  starting transfers between devices  10.3 us (3%)
    scatter-add x4, other arithmetic, advance(): return (summed.at[targets].add(message, mode='drop'), None)  57.9 us
    gather x4, local copies, waits for them, and re-layouts, advance(): jnp.take(receiver_term, jnp.minimum(targets, count - 1), axis=0)  40.9 us
    gather x3, local copies, waits for them, and re-layouts, fetch(): return jnp.take(table, picked, axis=0).astype(jnp.float32)  37.6 us
    reduce_scatter x1, waiting for transfers between devices, body(): lax.psum_scatter(partial_value.astype(jnp.bfloat16), 'gx', scatter_dimens...  26.2 us
    dot_general x4, matrix products, advance(): message = jnp.dot(hidden, weight_out, preferred_element_type=jnp.float32)  17 us
    scatter-add x1, other arithmetic, body(): jnp.zeros((members * coarse_rows,), jnp.float32).at[parent].add(1.0)  14.7 us
    scatter-add x1, other arithmetic, body(): partial_value = jnp.zeros((members * coarse_rows, width), jnp.float32).at...  13 us
    all_gather x1, blocking collectives, body(): whole = lax.all_gather(coarse_two, 'gx', axis=0, tiled=True)  12.4 us
  transfers between devices with their start and end apart: 5, of which 1 were waited for; matrix products, arithmetic and copies ran while one was open for 12% of the time, Pallas kernels for 0%

profile of v1, /device:TPU:0, one launch (start us, length us, event | category | flops | bytes accessed | tf_op | source)
XLA Modules:
  0.0 361.5 jit_solution(15277060333593748989)
XLA Ops:
  12.6 5.6 %collective-permute-start = (bf16[512,256]{1,0:T(8,128)(2,1)}, bf16[512,256]{1,0:T(8,128)(2,1)}, u32[]{:S(2)}, u32[]{:S(2)}) collective-permute-start(bf16[512,256]{1,0:T(8,128)(2,1)} %broadcast_select_fusion.3), channel_id=1, source_target_pairs={{0,8},{8,16},{16,24},{1,9},{9,17},{17,25},{2,10},{10,18},{18,26},{... | collective-permute-start | bytes 786440 | tf_op jit(solution)/shard_map/ppermute | solution.py:11
  25.1 2.2 collective-permute-start.2
  34.7 2.7 fusion.46
  41.0 14.7 %scatter_custom_fusion.2 = f32[1024]{0:T(1024)S(1)} fusion(s32[2048]{0:T(1024)S(1)} %get-tuple-element.111, f32[2048]{0:T(1024)S(1)} %broadcast.313, f32[]{:T(128)} %constant.136.clone.1), kind=kCustom, calls=%fused_computation.167 | custom fusion | flops 2048 | bytes 4100 | tf_op jit(solution)/shard_map/scatter-add | solution.py:113
  55.8 2.3 scatter_custom_fusion.5
  59.2 11.6 %all-reduce.1 = (bf16[1024]{0:T(1024)(128)(2,1)}, bf16[128]{0:T(256)(128)(2,1)S(1)}) all-reduce(bf16[1024]{0:T(1024)(128)(2,1)S(1)} %convert_element_type.147, bf16[128]{0:T(256)(128)(2,1)S(1)} %convert_element_type.162), channel_id=4, replica_groups=mesh['gx'=4,'gy'=8] {'gx'}, use_global_device_ids=true, to_apply=%region_8.10.clone | all-reduce | flops 1152 | bytes 4608
  72.6 2.3 copy.34
  80.7 132.0 %while.2 = (s32[]{:T(128)}, f32[2048,256]{1,0:T(8,128)S(1)}, s32[2]{0:T(128)S(1)}, s32[8192]{0:T(1024)S(1)}, s32[8192]{0:T(1024)S(1)}, /*index=5*/bf16[4096,256]...) while((s32[]{:T(128)}, f32[2048,256]{1,0:T(8,128)S(1)}, ...), condition=%wide.region_2.4_spmd, body=%wide.region_0.3_spmd.sunk | while | flops 548507648 | bytes 30195924 | solution.py:40
  82.0 17.0 %gather_fusion = bf16[4096,256]{1,0:T(8,128)(2,1)} fusion(bf16[2048,256]{1,0:T(8,128)(2,1)S(1)} %get-tuple-element.235, s32[4096]{0:T(1024)S(1)} %get-tuple-element.201), kind=kCustom, calls=%fused_computation.2.clone.1 | custom fusion | bytes 4210688 | tf_op jit(solution)/shard_map/while/body/eval_jaxpr/jit(_take)/gather | solution.py:32
  99.0 17.8 %gather_fusion.1 = bf16[4096,256]{1,0:T(8,128)(2,1)} fusion(bf16[4096,256]{1,0:T(8,128)(2,1)} %get-tuple-element.234, s32[4096]{0:T(1024)S(1)} %get-tuple-element.202), kind=kCustom, calls=%fused_computation.1.clone.1 | custom fusion | bytes 4210688 | tf_op jit(solution)/shard_map/while/body/eval_jaxpr/jit(_take)/gather | solution.py:62
  116.9 6.1 %fusion.123 = f32[4096,256]{1,0:T(8,128)} fusion(bf16[256,256]{1,0:T(8,128)(2,1)S(1)} %copy-done.6, bf16[4096,256]{1,0:T(8,128)(2,1)} %gather_fusion, bf16[4096,256]{1,0:T(8,128)(2,1)} %gather_fusion.1, pred[4096]{0:T(1024)(128)(4,1)S(1)} %get-tuple-element.203, pred[4096]{0:T(1024)(128)(4,1)S(1)} %get-tuple-element.204), kind=kOutput, calls=%fused_computation.20.clone.1 | convolution fusion | flops 547356672 | bytes 8527872 | tf_op jit(solution)/shard_map/while/body/eval_jaxpr/dot_general | solution.py:36
  123.0 23.6 %scatter_fusion = f32[2048,256]{1,0:T(8,128)S(1)} fusion(f32[2048,256]{1,0:T(8,128)S(1)} %get-tuple-element.218, s32[4096]{0:T(1024)S(1)} %get-tuple-element.200, f32[4096,256]{1,0:T(8,128)} %fusion.123), kind=kCustom, calls=%fused_computation.12.clone.1 | custom fusion | flops 1048576 | bytes 12599296 | tf_op jit(solution)/shard_map/while/body/eval_jaxpr/scatter-add | solution.py:37
  148.0 17.0 %gather_fusion = bf16[4096,256]{1,0:T(8,128)(2,1)} fusion(bf16[2048,256]{1,0:T(8,128)(2,1)S(1)} %get-tuple-element.235, s32[4096]{0:T(1024)S(1)} %get-tuple-element.201), kind=kCustom, calls=%fused_computation.2.clone.1 | custom fusion | bytes 4210688 | tf_op jit(solution)/shard_map/while/body/eval_jaxpr/jit(_take)/gather | solution.py:32
  165.0 17.8 %gather_fusion.1 = bf16[4096,256]{1,0:T(8,128)(2,1)} fusion(bf16[4096,256]{1,0:T(8,128)(2,1)} %get-tuple-element.234, s32[4096]{0:T(1024)S(1)} %get-tuple-element.202), kind=kCustom, calls=%fused_computation.1.clone.1 | custom fusion | bytes 4210688 | tf_op jit(solution)/shard_map/while/body/eval_jaxpr/jit(_take)/gather | solution.py:62
  182.9 6.1 %fusion.123 = f32[4096,256]{1,0:T(8,128)} fusion(bf16[256,256]{1,0:T(8,128)(2,1)S(1)} %copy-done.6, bf16[4096,256]{1,0:T(8,128)(2,1)} %gather_fusion, bf16[4096,256]{1,0:T(8,128)(2,1)} %gather_fusion.1, pred[4096]{0:T(1024)(128)(4,1)S(1)} %get-tuple-element.203, pred[4096]{0:T(1024)(128)(4,1)S(1)} %get-tuple-element.204), kind=kOutput, calls=%fused_computation.20.clone.1 | convolution fusion | flops 547356672 | bytes 8527872 | tf_op jit(solution)/shard_map/while/body/eval_jaxpr/dot_general | solution.py:36
  189.0 23.6 %scatter_fusion = f32[2048,256]{1,0:T(8,128)S(1)} fusion(f32[2048,256]{1,0:T(8,128)S(1)} %get-tuple-element.218, s32[4096]{0:T(1024)S(1)} %get-tuple-element.200, f32[4096,256]{1,0:T(8,128)} %fusion.123), kind=kCustom, calls=%fused_computation.12.clone.1 | custom fusion | flops 1048576 | bytes 12599296 | tf_op jit(solution)/shard_map/while/body/eval_jaxpr/scatter-add | solution.py:37
  212.6 3.8 %fusion.99 = (f32[2048]{0:T(1024)S(1)}, f32[2048,256]{0,1:T(8,128)}) fusion(bf16[6,256,256]{2,1,0:T(8,128)(2,1)} %param.22, f32[2048,256]{1,0:T(8,128)} %fusion.46, f32[2048,256]{1,0:T(8,128)S(1)} %get-tuple-element.85), kind=kOutput, calls=%fused_computation.195 | convolution fusion | flops 541063168 | bytes 6561792 | tf_op jit(solution)/shard_map/dot_general | solution.py:50
  222.3 13.0 %scatter_custom_fusion.1 = f32[1024,256]{1,0:T(8,128)} fusion(s32[2048]{0:T(1024)S(1)} %copy-done.10, f32[2048,256]{1,0:T(8,128)} %copy.35, f32[]{:T(128)} %constant.136.clone.1), kind=kCustom, calls=%fused_computation.52 | custom fusion | flops 524288 | bytes 1049088 | tf_op jit(solution)/shard_map/scatter-add | solution.py:111
  235.3 2.2 copy.36
  238.4 26.2 %reduce-scatter.2.cloned.1.call-done = bf16[256,256]{0,1:T(8,128)(2,1)} async-done(((bf16[1024,256]{0,1:T(8,128)(2,1)}), bf16[256,256]{0,1:T(8,128)(2,1)}) %reduce-scatter.2.cloned.1.call-update) | async-done | bytes 131088 | tf_op jit(solution)/shard_map/reduce_scatter | solution.py:115
  265.8 10.5 %all_gather.12 = bf16[1024,256]{1,0:T(8,128)(2,1)S(1)} all-gather(bf16[256,256]{1,0:T(8,128)(2,1)S(1)} %convolution_convert_fusion.3), channel_id=1, replica_groups=mesh['gx'=4,'gy'=8] {'gx'}, dimensions={0}, use_global_device_ids=true | all-gather | bytes 655360 | tf_op jit(solution)/shard_map/all_gather | solution.py:125
  276.3 3.9 %gather_fusion.2 = bf16[1024,256]{1,0:T(8,128)(2,1)S(1)} fusion(bf16[1024,256]{1,0:T(8,128)(2,1)S(1)} %all_gather.12, s32[1024]{0:T(1024)S(1)} %get-tuple-element.141), kind=kCustom, calls=%fused_computation.8 | custom fusion | bytes 1052672 | tf_op jit(solution)/shard_map/jit(_take)/gather | solution.py:127
  281.4 5.0 %gather_fusion.3 = bf16[1024,256]{1,0:T(8,128)(2,1)} fusion(bf16[256,256]{1,0:T(8,128)(2,1)S(1)} %convolution_convert_fusion.2, s32[1024]{0:T(1024)S(1)} %get-tuple-element.140), kind=kCustom, calls=%fused_computation.9 | custom fusion | bytes 1052672 | tf_op jit(solution)/shard_map/while/body/eval_jaxpr/jit(_take)/gather | solution.py:32
  286.4 2.7 fusion.15
  289.0 6.6 %scatter_custom_fusion.3 = f32[256,256]{1,0:T(8,128)S(1)} fusion(s32[1024]{0:T(1024)S(1)} %bitcast.139, f32[1024,256]{1,0:T(8,128)} %fusion.15, f32[]{:T(128)} %constant.136.clone.1), kind=kCustom, calls=%fused_computation.112 | custom fusion | flops 262144 | bytes 262656 | tf_op jit(solution)/shard_map/while/body/eval_jaxpr/scatter-add | solution.py:37
  300.7 7.8 %all-gather = bf16[512,256]{1,0:T(8,128)(2,1)S(1)} all-gather(bf16[128,256]{1,0:T(8,128)(2,1)S(1)} %convert_element_type.160), channel_id=2, replica_groups=mesh['gx'=4,'gy'=8] {'gx'}, dimensions={0}, use_global_device_ids=true | all-gather | bytes 327680 | tf_op jit(solution)/shard_map/all_gather | solution.py:150
  318.0 4.1 %scatter_custom_fusion.6 = f32[128,256]{1,0:T(8,128)S(1)} fusion(s32[512]{0:T(512)} %bitcast.144, f32[512,256]{1,0:T(8,128)} %fusion.21, f32[]{:T(128)} %constant.136.clone.1), kind=kCustom, calls=%fused_computation.123 | custom fusion | flops 131072 | bytes 131584 | tf_op jit(solution)/shard_map/while/body/eval_jaxpr/scatter-add | solution.py:37
  325.2 12.4 %all_gather.15 = bf16[1024,256]{0,1:T(8,128)(2,1)S(1)} all-gather(bf16[256,256]{0,1:T(8,128)(2,1)S(1)} %add_convert_fusion.2), channel_id=1, replica_groups=mesh['gx'=4,'gy'=8] {'gx'}, dimensions={0}, use_global_device_ids=true | all-gather | bytes 655360 | tf_op jit(solution)/shard_map/all_gather | solution.py:167
  337.8 9.1 %gather_fusion.5 = bf16[2048,256]{1,0:T(8,128)(2,1)} fusion(bf16[1024,256]{1,0:T(8,128)(2,1)S(1)} %copy.39, s32[2048]{0:T(1024)S(1)} %broadcast_clamp_fusion), kind=kCustom, calls=%fused_computation.11 | custom fusion | bytes 2105344 | tf_op jit(solution)/shard_map/jit(_take)/gather | solution.py:168
  346.8 2.3 copy.40
  349.1 2.5 add_convert_fusion
  351.6 2.3 copy.41
  (172 shorter events, 60.0 us)
Async XLA Ops:
  7.2 257.4 %reduce-scatter.2.cloned.1.call-start = ((), (), s32[]{:S(2)}) async-start(), calls=%async_computation.1 | async-start | bytes 655360 | tf_op jit(solution)/shard_map/reduce_scatter | solution.py:115
  12.6 63.5 %collective-permute-start = (bf16[512,256]{1,0:T(8,128)(2,1)}, bf16[512,256]{1,0:T(8,128)(2,1)}, u32[]{:S(2)}, u32[]{:S(2)}) collective-permute-start(bf16[512,256]{1,0:T(8,128)(2,1)} %broadcast_select_fusion.3), channel_id=1, source_target_pairs={{0,8},{8,16},{16,24},{1,9},{9,17},{17,25},{2,10},{10,18},{18,26},{... | collective-permute-start | bytes 786440 | tf_op jit(solution)/shard_map/ppermute | solution.py:11
  21.0 56.2 %collective-permute-start.1 = (bf16[512,256]{1,0:T(8,128)(2,1)}, bf16[512,256]{1,0:T(8,128)(2,1)}, u32[]{:S(2)}, u32[]{:S(2)}) collective-permute-start(bf16[512,256]{1,0:T(8,128)(2,1)} %broadcast_select_fusion.2), channel_id=1, source_target_pairs={{8,0},{16,8},{24,16},{9,1},{17,9},{25,17},{10,2},{18,10},{26,18},{... | collective-permute-start | bytes 786440 | tf_op jit(solution)/shard_map/ppermute | solution.py:11
  25.1 53.0 %collective-permute-start.2 = (bf16[512,256]{1,0:T(8,128)(2,1)}, bf16[512,256]{1,0:T(8,128)(2,1)}, u32[]{:S(2)}, u32[]{:S(2)}) collective-permute-start(bf16[512,256]{1,0:T(8,128)(2,1)} %broadcast_select_fusion.1), channel_id=1, source_target_pairs={{0,1},{1,2},{2,3},{3,4},{4,5},{5,6},{6,7},{8,9},{9,10},{10,11},{11... | collective-permute-start | bytes 786440 | tf_op jit(solution)/shard_map/ppermute | solution.py:11
  29.2 5.5 %copy-start.1 = (bf16[2048,256]{1,0:T(8,128)(2,1)S(1)}, bf16[2048,256]{1,0:T(8,128)(2,1)}, u32[]{:S(2)}) copy-start(bf16[2048,256]{1,0:T(8,128)(2,1)} %param.21) | copy-start | bytes 3145732
  30.1 49.0 %collective-permute-start.3 = (bf16[512,256]{1,0:T(8,128)(2,1)}, bf16[512,256]{1,0:T(8,128)(2,1)S(1)}, u32[]{:S(2)}, u32[]{:S(2)}) collective-permute-start(bf16[512,256]{1,0:T(8,128)(2,1)} %broadcast_select_fusion), channel_id=1, source_target_pairs={{1,0},{2,1},{3,2},{4,3},{5,4},{6,5},{7,6},{9,8},{10,9},{11,10},{12... | collective-permute-start | bytes 786440 | tf_op jit(solution)/shard_map/ppermute | solution.py:11
  33.0 4.4 %copy-start.7 = (s32[1,1024]{1,0:T(1,128)S(1)}, s32[1,1024]{1,0:T(1,128)}, u32[]{:S(2)}) copy-start(s32[1,1024]{1,0:T(1,128)} %param.31) | copy-start | bytes 12292
  33.0 5.5 %copy-start.22 = (s32[1,512]{1,0:T(1,128)S(1)}, s32[1,512]{1,0:T(1,128)}, u32[]{:S(2)}) copy-start(s32[1,512]{1,0:T(1,128)} %param.35) | copy-start | bytes 6148
  33.1 5.6 %copy-start.21 = (s32[1,512]{1,0:T(1,128)S(1)}, s32[1,512]{1,0:T(1,128)}, u32[]{:S(2)}) copy-start(s32[1,512]{1,0:T(1,128)} %param.34) | copy-start | bytes 6148
  33.1 6.7 %copy-start.27 = (f32[3,256]{1,0:T(4,128)S(1)}, f32[3,256]{1,0:T(4,128)}, u32[]{:S(2)}) copy-start(f32[3,256]{1,0:T(4,128)} %param.25) | copy-start | bytes 9220
  33.1 7.3 %copy-start.19 = (s32[2048,1]{0,1:T(1,128)S(1)}, s32[2048,1]{0,1:T(1,128)}, u32[]{:S(2)}) copy-start(s32[2048,1]{0,1:T(1,128)} %param.29) | copy-start | bytes 24580
  33.1 7.3 %copy-start.20 = (s32[2048]{0:T(1024)S(1)}, s32[2048]{0:T(1024)}, u32[]{:S(2)}) copy-start(s32[2048]{0:T(1024)} %param.30) | copy-start | bytes 24580
  33.1 22.6 %copy-start.28 = (s32[1,256]{1,0:T(1,128)S(1)}, s32[1,256]{1,0:T(1,128)}, u32[]{:S(2)}) copy-start(s32[1,256]{1,0:T(1,128)} %param.33) | copy-start | bytes 3076
  33.1 25.0 %copy-start.11 = (s32[1,1024]{1,0:T(1,128)S(1)}, s32[1,1024]{1,0:T(1,128)}, u32[]{:S(2)}) copy-start(s32[1,1024]{1,0:T(1,128)} %param.32) | copy-start | bytes 12292
  34.7 40.1 %copy-start.33 = (u32[32]{0:T(128)S(1)}, u32[32]{0:T(128)}, u32[]{:S(2)}) copy-start(u32[32]{0:T(128)} %constant.211) | copy-start | bytes 388
  41.0 38.1 %copy-start.9 = (s32[2048]{0:T(1024)}, s32[2048]{0:T(1024)S(1)}, u32[]{:S(2)}) copy-start(s32[2048]{0:T(1024)S(1)} %get-tuple-element.111) | copy-start | bytes 24580
  55.7 23.4 %copy-start.25 = (s32[256,1]{0,1:T(1,128)}, s32[256,1]{0,1:T(1,128)S(1)}, u32[]{:S(2)}) copy-start(s32[256,1]{0,1:T(1,128)S(1)} %compare_select_fusion.10) | copy-start | bytes 3076
  76.1 4.5 %copy-start.3 = (s32[1,1,8192]{2,1,0:T(1,128)S(1)}, s32[1,1,8192]{2,1,0:T(1,128)}, u32[]{:S(2)}) copy-start(s32[1,1,8192]{2,1,0:T(1,128)} %param.28) | copy-start | bytes 98308
  76.1 4.5 %copy-start.4 = (s32[1,1,8192]{2,1,0:T(1,128)S(1)}, s32[1,1,8192]{2,1,0:T(1,128)}, u32[]{:S(2)}) copy-start(s32[1,1,8192]{2,1,0:T(1,128)} %param.27) | copy-start | bytes 98308
  99.0 17.9 %copy-start.6 = (bf16[256,256]{1,0:T(8,128)(2,1)S(1)}, bf16[256,256]{1,0:T(8,128)(2,1)}, u32[]{:S(2)}) copy-start(bf16[256,256]{1,0:T(8,128)(2,1)} %get-tuple-element.236) | copy-start | bytes 393220 | tf_op jit(solution)/shard_map/while
  165.0 17.9 %copy-start.6 = (bf16[256,256]{1,0:T(8,128)(2,1)S(1)}, bf16[256,256]{1,0:T(8,128)(2,1)}, u32[]{:S(2)}) copy-start(bf16[256,256]{1,0:T(8,128)(2,1)} %get-tuple-element.236) | copy-start | bytes 393220 | tf_op jit(solution)/shard_map/while
  222.3 16.0 %copy-start.8 = (s32[1,1024]{1,0:T(1,128)S(1)}, s32[1,1024]{1,0:T(1,128)}, u32[]{:S(2)}) copy-start(s32[1,1024]{1,0:T(1,128)} %param.31) | copy-start | bytes 12292
  222.3 16.0 %copy-start.13 = (s32[1,1024]{1,0:T(1,128)S(1)}, s32[1,1024]{1,0:T(1,128)}, u32[]{:S(2)}) copy-start(s32[1,1024]{1,0:T(1,128)} %broadcast_clamp_fusion.3) | copy-start | bytes 12292
  222.3 16.0 %copy-start.14 = (s32[1,1024]{1,0:T(1,128)S(1)}, s32[1,1024]{1,0:T(1,128)}, u32[]{:S(2)}) copy-start(s32[1,1024]{1,0:T(1,128)} %broadcast_minimum_fusion) | copy-start | bytes 12292
  222.3 16.1 %copy-start.12 = (s32[1,1024]{1,0:T(1,128)S(1)}, s32[1,1024]{1,0:T(1,128)}, u32[]{:S(2)}) copy-start(s32[1,1024]{1,0:T(1,128)} %param.32) | copy-start | bytes 12292
  222.3 16.1 %copy-start.15 = (s32[1024,1]{0,1:T(1,128)S(1)}, s32[1024,1]{0,1:T(1,128)}, u32[]{:S(2)}) copy-start(s32[1024,1]{0,1:T(1,128)} %compare_select_fusion.4) | copy-start | bytes 12292
  289.0 9.2 %copy-start.24 = (f32[1,256]{1,0:T(1,128)S(1)}, f32[1,256]{1,0:T(1,128)}, u32[]{:S(2)}) copy-start(f32[1,256]{1,0:T(1,128)} %get-tuple-element.123) | copy-start | bytes 3076
  296.8 11.7 %copy-start.30 = (f32[128]{0:T(128)S(1)}, f32[128]{0:T(128)}, u32[]{:S(2)}) copy-start(f32[128]{0:T(128)} %convert_maximum_fusion.1) | copy-start | bytes 1540
  298.3 13.6 %copy-start.17 = (s32[1024]{0:T(1024)S(1)}, s32[1024]{0:T(1024)}, u32[]{:S(2)}) copy-start(s32[1024]{0:T(1024)} %get-tuple-element.135) | copy-start | bytes 12292
  308.5 5.4 %copy-start.16 = (s32[1024]{0:T(1024)S(1)}, s32[1024]{0:T(1024)}, u32[]{:S(2)}) copy-start(s32[1024]{0:T(1024)} %get-tuple-element.134) | copy-start | bytes 12292
  315.9 7.8 %copy-start.23 = (f32[1,256]{1,0:T(1,128)S(1)}, f32[1,256]{1,0:T(1,128)}, u32[]{:S(2)}) copy-start(f32[1,256]{1,0:T(1,128)} %get-tuple-element.121) | copy-start | bytes 3076
  318.0 7.2 %copy-start.29 = (pred[256]{0:T(512)(128)(4,1)S(1)}, pred[256]{0:T(512)(128)(4,1)}, u32[]{:S(2)}) copy-start(pred[256]{0:T(512)(128)(4,1)} %compare_and_fusion.11) | copy-start | bytes 772
  (8 other events, 21.8 us)
Sparse Core Ops, SparseCore 0:
  237.7 26.8 reduce-scatter.1
